TPU v7x, 32 devices: a whole 2x2x4 slice. The times are simulated.
32 devices in a mesh: seq: 8 (over z, x), wsh: 4 (over y, core).
Axes of the slice: x: 2, y: 2, z: 4, core: 2. Of those that a mesh axis runs over, the one named last changes fastest.
Arguments:
- tokens_in: bfloat16 [4, 4096, 1024], P('wsh', 'seq'), may hold values from -6 to 6
- out_grad: bfloat16 [4, 4096, 1024], P('wsh', 'seq'), may hold values from -6 to 6
- deal_order: int32 [8], replicated, may hold values from 0 to 7, each once
- seq_lengths: int32 [4, 4], P('wsh'), may hold values from 1 to 2048, 4096 in all within a row
- weights: bfloat16 [1024, 17920], P('wsh'), may hold values from -0.1875 to 0.1875
- norm_gains: bfloat16 [2, 1024], P(None, 'wsh'), may hold values from 0.5 to 1.5
- conv_kernel: bfloat16 [3, 1024], P(None, 'wsh'), may hold values from -3 to 3
- vector_state: float32 [5, 1024], P(None, 'wsh'), may hold values from 0.2 to 5
- kron_stats: float32 [2, 1120, 128, 128], P(None, 'wsh', 'seq'), may hold values from -6 to 6
- kron_roots: float32 [2, 1120, 128, 128], P(None, 'wsh', 'seq'), as said below
Outputs:
- block_out: bfloat16 [4, 4096, 1024], P('wsh', 'seq')
- input_grad: bfloat16 [4, 4096, 1024], P('wsh', 'seq')
- weight_grad: float32 [1024, 17920], P('wsh')
- vector_grad: float32 [5, 1024], P(None, 'wsh')
- vector_state_new: float32 [5, 1024], P(None, 'wsh')
- vector_update: float32 [5, 1024], P(None, 'wsh')
- kron_stats_new: float32 [2, 1120, 128, 128], P(None, 'wsh', 'seq')
- weight_update: float32 [1120, 128, 128], P('wsh', 'seq')
Inputs may be any that keep to these rules, and one draw needn't show every extreme that they name: `deal_order`: a permutation of 0 to 7. `seq_lengths`: each row sums to 4096; in every pack the longest sequence has exactly 2048 tokens. `kron_roots`: each block has a dominant diagonal between 0.5 and 2.
All inputs are finite; a program needn't handle non-finite values.
Results may differ from a plain program's by a relative error of at most 0.025.
Values may be sent and summed in bfloat16 or wider, within the bound.
A program may use at most 320 MiB of HBM per device.

v0:
```python
import jax
import jax.numpy as jnp
from jax import lax
from jax.sharding import PartitionSpec as P

D = 1024
FF = 4608
BLK = 128
EPS = 1e-05
BETA = 0.5
BETA_VEC = 0.5
LEARN = 0.03
LEARN_VEC = 0.05
HIGH = lax.Precision.HIGHEST


def passed_along(block, axis, distance):
    devices = range(lax.axis_size(axis))
    route = [(i - distance, i) for i in devices if i - distance in devices]
    return lax.ppermute(block, axis, route)


def seq_positions(lengths_row, first, count):
    starts = jnp.cumsum(lengths_row) - lengths_row
    rows_at = first + jnp.arange(count, dtype=jnp.int32)
    begin = jnp.max(jnp.where(starts[None, :] <= rows_at[:, None], starts[None, :], 0), axis=1)
    return rows_at - begin


def rms_scale(values):
    return lax.rsqrt(jnp.mean(values * values, axis=1, keepdims=True) + EPS)


def norm_back(upstream, values, scale, gain):
    scaled = upstream * gain
    inner = jnp.mean(scaled * values, axis=1, keepdims=True)
    return (
        scale * scaled - values * scale * scale * scale * inner,
        jnp.sum(upstream * values * scale, axis=0),
    )


def contract_rows(left, right):
    return lax.dot_general(
        left, right, (((0,), (0,)), ((), ())), preferred_element_type=jnp.float32
    )


def contract_cols(left, right):
    return lax.dot_general(
        left, right, (((1,), (1,)), ((), ())), preferred_element_type=jnp.float32
    )


def shards(
    tokens_in,
    out_grad,
    deal_order,
    seq_lengths,
    weights,
    norm_gains,
    conv_kernel,
    vector_state,
    kron_stats,
    kron_roots,
):
    n_seq = lax.axis_size("seq")
    n_wsh = lax.axis_size("wsh")
    rows = tokens_in.shape[1]
    unit = rows // n_seq
    arrived = (
        lax.all_to_all(
            tokens_in.reshape(n_seq, unit, D), "seq", split_axis=0, concat_axis=0, tiled=True
        ),
        lax.all_to_all(
            out_grad.reshape(n_seq, unit, D), "seq", split_axis=0, concat_axis=0, tiled=True
        ),
    )
    x_bf = jnp.take(arrived[0], deal_order, axis=0).reshape(rows, D)
    dy_bf = jnp.take(arrived[1], deal_order, axis=0).reshape(rows, D)
    full_w, gains_bf, kernel_bf = (
        lax.all_gather(weights, "wsh", axis=0, tiled=True),
        lax.all_gather(norm_gains, "wsh", axis=1, tiled=True),
        lax.all_gather(conv_kernel, "wsh", axis=1, tiled=True),
    )
    gains = gains_bf.astype(jnp.float32)
    kernel = kernel_bf.astype(jnp.float32)
    first_row = lax.axis_index("seq") * rows
    pos = seq_positions(seq_lengths[0], first_row, rows + 2)
    masks = [(pos >= 2 - k).astype(jnp.float32)[:, None] for k in range(3)]
    xf = x_bf.astype(jnp.float32)
    scale_one = rms_scale(xf)
    xn = (xf * scale_one * gains[0]).astype(jnp.bfloat16)
    proj = jnp.dot(xn, full_w[:, : 3 * D], preferred_element_type=jnp.float32)
    b_part = proj[:, :D]
    c_part = proj[:, D : 2 * D]
    x_part = proj[:, 2 * D :]
    conv_in = b_part * x_part
    prev = passed_along(conv_in[rows - 2 :], "seq", 1)
    ext = jnp.concatenate([prev, conv_in], axis=0)
    conv = (
        kernel[0] * masks[0][:rows] * ext[0:rows]
        + kernel[1] * masks[1][:rows] * ext[1 : rows + 1]
        + kernel[2] * masks[2][:rows] * ext[2 : rows + 2]
    )
    yc = (c_part * conv).astype(jnp.bfloat16)
    hidden_sum = xf + jnp.dot(yc, full_w[:, 3 * D : 4 * D], preferred_element_type=jnp.float32)
    scale_two = rms_scale(hidden_sum)
    hn = (hidden_sum * scale_two * gains[1]).astype(jnp.bfloat16)
    gate_up = jnp.dot(hn, full_w[:, 4 * D : 4 * D + 2 * FF], preferred_element_type=jnp.float32)
    gate = gate_up[:, :FF]
    upper = gate_up[:, FF:]
    sig = jax.nn.sigmoid(gate)
    act = (gate * sig * upper).astype(jnp.bfloat16)
    ffn = contract_cols(act, full_w[:, 4 * D + 2 * FF :])
    result = (hidden_sum + ffn).astype(jnp.bfloat16)
    g_down = contract_rows(dy_bf, act)
    d_act = jnp.dot(dy_bf, full_w[:, 4 * D + 2 * FF :], preferred_element_type=jnp.float32)
    d_gate = d_act * upper * sig * (1.0 + gate * (1.0 - sig))
    d_upper = d_act * gate * sig
    d_gu = jnp.concatenate([d_gate, d_upper], axis=1).astype(jnp.bfloat16)
    g_gu = contract_rows(hn, d_gu)
    d_hn = contract_cols(d_gu, full_w[:, 4 * D : 4 * D + 2 * FF])
    d_norm_two, g_gain_two = norm_back(d_hn, hidden_sum, scale_two, gains[1])
    d_hidden = dy_bf.astype(jnp.float32) + d_norm_two
    d_mix = d_hidden.astype(jnp.bfloat16)
    g_out = contract_rows(yc, d_mix)
    d_yc = contract_cols(d_mix, full_w[:, 3 * D : 4 * D])
    d_c = d_yc * conv
    d_conv = d_yc * c_part
    after = passed_along(d_conv[:2], "seq", -1)
    d_ext = jnp.concatenate([d_conv, after], axis=0)
    weighted = [d_ext * masks[k] for k in range(3)]
    d_bx = (
        kernel[2] * weighted[2][:rows]
        + kernel[1] * weighted[1][1 : rows + 1]
        + kernel[0] * weighted[0][2 : rows + 2]
    )
    g_taps = jnp.stack([jnp.sum(weighted[k][:rows] * ext[k : k + rows], axis=0) for k in range(3)])
    d_proj = jnp.concatenate([d_bx * x_part, d_c, d_bx * b_part], axis=1).astype(jnp.bfloat16)
    g_in = contract_rows(xn, d_proj)
    d_xn = contract_cols(d_proj, full_w[:, : 3 * D])
    d_norm_one, g_gain_one = norm_back(d_xn, xf, scale_one, gains[0])
    d_input = (d_hidden + d_norm_one).astype(jnp.bfloat16)
    g_vec = jnp.concatenate([g_gain_one[None], g_gain_two[None], g_taps], axis=0)
    inverse = jnp.argsort(deal_order)
    leaving = (
        jnp.take(result.reshape(n_seq, unit, D), inverse, axis=0),
        jnp.take(d_input.reshape(n_seq, unit, D), inverse, axis=0),
    )
    returned = (
        lax.all_to_all(leaving[0], "seq", split_axis=0, concat_axis=0, tiled=True),
        lax.all_to_all(leaving[1], "seq", split_axis=0, concat_axis=0, tiled=True),
    )
    summed = (
        lax.psum_scatter(g_in.astype(jnp.bfloat16), "wsh", scatter_dimension=0, tiled=True).astype(
            jnp.float32
        ),
        lax.psum_scatter(g_out.astype(jnp.bfloat16), "wsh", scatter_dimension=0, tiled=True).astype(
            jnp.float32
        ),
        lax.psum_scatter(g_gu.astype(jnp.bfloat16), "wsh", scatter_dimension=0, tiled=True).astype(
            jnp.float32
        ),
        lax.psum_scatter(
            g_down.astype(jnp.bfloat16), "wsh", scatter_dimension=0, tiled=True
        ).astype(jnp.float32),
        lax.psum_scatter(g_vec.astype(jnp.bfloat16), "wsh", scatter_dimension=1, tiled=True).astype(
            jnp.float32
        ),
    )
    summed = (
        lax.psum(summed[0].astype(jnp.bfloat16), "seq").astype(jnp.float32),
        lax.psum(summed[1].astype(jnp.bfloat16), "seq").astype(jnp.float32),
        lax.psum(summed[2].astype(jnp.bfloat16), "seq").astype(jnp.float32),
        lax.psum(summed[3].astype(jnp.bfloat16), "seq").astype(jnp.float32),
        lax.psum(summed[4].astype(jnp.bfloat16), "seq").astype(jnp.float32),
    )
    grad_scale = lax.rsqrt(jnp.asarray(rows * n_seq * n_wsh, jnp.float32))
    grad_shard = jnp.concatenate([summed[0], summed[1], summed[2], summed[3]], axis=1) * grad_scale
    vec_grad = summed[4] * grad_scale
    state_new = BETA_VEC * vector_state + (1.0 - BETA_VEC) * vec_grad * vec_grad
    vec_update = -LEARN_VEC * vec_grad * lax.rsqrt(state_new)
    nrow_blocks = grad_shard.shape[0] // BLK
    ncol_blocks = grad_shard.shape[1] // BLK
    grad_blocks = (
        grad_shard.reshape(nrow_blocks, BLK, ncol_blocks, BLK)
        .transpose(0, 2, 1, 3)
        .reshape(nrow_blocks * ncol_blocks, BLK, BLK)
    )
    share = BLK // n_seq
    first_block_row = lax.axis_index("seq") * share
    block_rows = lax.dynamic_slice_in_dim(grad_blocks, first_block_row, share, 1)
    block_cols = lax.dynamic_slice_in_dim(grad_blocks, first_block_row, share, 2)
    left_term = jnp.einsum("nij,nkj->nik", block_rows, grad_blocks, precision=HIGH)
    right_term = jnp.einsum("nji,njk->nik", block_cols, grad_blocks, precision=HIGH)
    stats_new = jnp.stack(
        [
            BETA * kron_stats[0] + (1.0 - BETA) * left_term / BLK,
            BETA * kron_stats[1] + (1.0 - BETA) * right_term / BLK,
        ]
    )
    right_full = lax.all_gather(
        kron_roots[1].astype(jnp.bfloat16), "seq", axis=1, tiled=True
    ).astype(jnp.float32)
    left_mul = jnp.einsum("nij,njk->nik", kron_roots[0], grad_blocks, precision=HIGH)
    update = -LEARN * jnp.einsum("nij,njk->nik", left_mul, right_full, precision=HIGH)
    return (
        returned[0].reshape(1, rows, D),
        returned[1].reshape(1, rows, D),
        grad_shard,
        vec_grad,
        state_new,
        vec_update,
        stats_new,
        update,
    )


def solution(mesh):
    return jax.shard_map(
        shards,
        mesh=mesh,
        in_specs=(
            P("wsh", "seq", None),
            P("wsh", "seq", None),
            P(),
            P("wsh", None),
            P("wsh", None),
            P(None, "wsh"),
            P(None, "wsh"),
            P(None, "wsh"),
            P(None, "wsh", "seq", None),
            P(None, "wsh", "seq", None),
        ),
        out_specs=(
            P("wsh", "seq", None),
            P("wsh", "seq", None),
            P("wsh", None),
            P(None, "wsh"),
            P(None, "wsh"),
            P(None, "wsh"),
            P(None, "wsh", "seq", None),
            P("wsh", "seq", None),
        ),
        check_vma=False,
    )
```

profile of v0, /device:TPU:0, one launch (start us, length us, event | category | flops | bytes accessed | tf_op | source)
XLA Modules:
  0.0 1136.9 jit_solution(3107054169689322003)
XLA Ops:
  7.2 0.7 all-gather.4.cloned.1.call-update
  7.9 7.4 all-to-all-start
  15.6 25.6 %all-to-all-done = bf16[8,64,1024]{2,1,0:T(8,128)(2,1)S(1)} async-done(((bf16[8,64,1024]{2,1,0:T(8,128)(2,1)}), bf16[8,64,1024]{2,1,0:T(8,128)(2,1)S(1)}, u32[]{:S(2)}, u32[]{:S(2)}) %all-to-all-start) | async-done | bytes 1048608 | tf_op jit(solution)/shard_map/all_to_all | solution.py:72
  41.1 4.3 all-to-all-start.2
  45.6 5.2 all_gather.12
  50.8 5.3 all_gather.14
  56.2 0.6 gather_fusion
  57.4 13.6 %all-to-all-done.2 = bf16[8,64,1024]{2,1,0:T(8,128)(2,1)} async-done(((bf16[8,64,1024]{2,1,0:T(8,128)(2,1)}), bf16[8,64,1024]{2,1,0:T(8,128)(2,1)}, u32[]{:S(2)}, u32[]{:S(2)}) %all-to-all-start.2) | async-done | bytes 1048608 | tf_op jit(solution)/shard_map/all_to_all | solution.py:75
  71.0 2.8 gather_fusion.2
  74.1 159.7 %all-gather.4.cloned.1.call-done = bf16[1024,17920]{1,0:T(8,128)(2,1)} async-done(((bf16[256,17920]{1,0:T(8,128)(2,1)}), bf16[1024,17920]{1,0:T(8,128)(2,1)}) %all-gather.4.cloned.1.call-update) | async-done | bytes 36700176 | tf_op jit(solution)/shard_map/all_gather | solution.py:82
  233.8 5.5 fusion.14
  239.3 0.5 slice_multiply_fusion.4
  239.8 3.7 collective-permute-start
  243.5 1.1 broadcast_select_fusion.2
  244.7 2.3 multiply_convert_fusion.7
  247.0 3.3 multiply_reduce_fusion.3
  250.3 18.3 %fusion.4 = f32[512,9216]{1,0:T(8,128)} fusion(bf16[1024,17920]{1,0:T(8,128)(2,1)} %all-gather.4.cloned.1.call-done, f32[512,1024]{1,0:T(8,128)S(1)} %get-tuple-element.51, f32[1024]{0:T(1024)S(1)} %bitcast.99, f32[512]{0:T(512)S(1)} %add_rsqrt_fusion.1), kind=kOutput, calls=%fused_computation.10 | convolution fusion | flops 9665249280 | bytes 39852032 | tf_op jit(solution)/shard_map/dot_general | solution.py:110
  268.6 17.8 %multiply_convert_fusion.1 = (bf16[512,4608]{1,0:T(8,128)(2,1)}, bf16[512,4608]{1,0:T(8,128)(2,1)}, bf16[512,4608]{1,0:T(8,128)(2,1)}) fusion(f32[512,9216]{1,0:T(8,128)} %fusion.4, bf16[512,1024]{1,0:T(8,128)(2,1)} %bitcast.86, bf16[1024,17920]{1,0:T(8,128)(2,1)} %all-gather.4.cloned.1.call-done), kind=kOutput, calls=%fused_computation.15 | convolution fusion | flops 4869586944 | bytes 43515904 | tf_op jit(solution)/shard_map/dot_general | solution.py:118
  286.4 16.0 %multiply_reduce_fusion.1 = (bf16[1024]{0:T(1024)(128)(2,1)S(1)}, f32[512]{0:T(512)S(1)}, f32[512,1024]{1,0:T(8,128)S(1)}) fusion(f32[512,1024]{1,0:T(8,128)} %copy-done.10, f32[512]{0:T(512)S(1)} %add_rsqrt_fusion.1, f32[1024]{0:T(1024)S(1)} %bitcast.100, bf16[1024,17920]{1,0:T(8,128)(2,1)} %all-gather.4.cloned.1.call-done, ...), kind=kOutput, calls=%fused_computation.75 | convolution fusion | flops 9685694464 | bytes 32516096 | tf_op jit(solution)/shard_map/dot_general | solution.py:50
  302.4 0.7 subtract_add_fusion
  303.2 1.5 copy-done.2
  304.7 2.6 convolution_convert_fusion.3
  307.4 3.7 fusion.42
  311.1 2.4 multiply_convert_fusion.4
  313.5 1.3 collective-permute-start.1
  314.8 4.5 collective-permute-done.1
  319.7 2.6 fusion.26
  322.3 0.5 multiply_convert_fusion.3
  323.3 0.5 copy-done.15
  324.2 5.7 convolution_convert_fusion.2
  330.0 1.1 copy-done.9
  331.1 9.8 convolution_convert_fusion.1
  341.0 1.5 copy-done.12
  342.6 17.8 %convolution_convert_fusion = bf16[1024,9216]{1,0:T(8,128)(2,1)} fusion(bf16[512,4608]{1,0:T(8,128)(2,1)} %get-tuple-element.32, bf16[512,4608]{1,0:T(8,128)(2,1)} %get-tuple-element.31, f32[512,1024]{1,0:T(8,128)S(1)} %copy-done.12, f32[1024]{0:T(1024)S(1)} %bitcast.102, f32[512]{0:T(512)S(1)} %add_rsqrt_fusion.1), kind=kOutput, calls=%fused_computation.7 | convolution fusion | flops 9693560832 | bytes 30414848 | tf_op jit(solution)/shard_map/dot_general | solution.py:44
  360.4 9.6 fusion.41
  370.1 0.6 concatenate.30
  370.8 30.0 %reduce-scatter.6.cloned.1.call-done = bf16[256,3072]{1,0:T(8,128)(2,1)} async-done(((bf16[1024,3072]{1,0:T(8,128)(2,1)}), bf16[256,3072]{1,0:T(8,128)(2,1)}) %reduce-scatter.6.cloned.1.call-update) | async-done | bytes 1572880 | tf_op jit(solution)/shard_map/reduce_scatter | solution.py:156
  400.9 81.0 %reduce-scatter.12.cloned.1.call-done = bf16[256,4608]{1,0:T(8,128)(2,1)} async-done(((bf16[1024,4608]{1,0:T(8,128)(2,1)}), bf16[256,4608]{1,0:T(8,128)(2,1)}) %reduce-scatter.12.cloned.1.call-update) | async-done | bytes 2359312 | tf_op jit(solution)/shard_map/reduce_scatter | solution.py:165
  481.9 140.3 %reduce-scatter.10.cloned.1.call-done = bf16[256,9216]{1,0:T(8,128)(2,1)} async-done(((bf16[1024,9216]{1,0:T(8,128)(2,1)}), bf16[256,9216]{1,0:T(8,128)(2,1)}) %reduce-scatter.10.cloned.1.call-update) | async-done | bytes 4718608 | tf_op jit(solution)/shard_map/reduce_scatter | solution.py:162
  622.3 2.8 slice.250
  625.1 1.0 sort.17
  626.1 9.9 add_convert_fusion
  636.0 3.0 gather_fusion.1
  638.9 3.3 fusion.37
  642.2 1.9 gather_fusion.3
  644.1 1.2 broadcast_select_fusion
  645.4 58.2 %all_to_all.20 = bf16[8,64,1024]{2,1,0:T(8,128)(2,1)S(1)} all-to-all(bf16[8,64,1024]{2,1,0:T(8,128)(2,1)S(1)} %get-tuple-element.49), channel_id=1, replica_groups=mesh['seq'=8,'wsh'=4] {'seq'}, dimensions={0} | all-to-all | bytes 2097152 | tf_op jit(solution)/shard_map/all_to_all | solution.py:152
  703.6 3.7 all-to-all-start.3
  707.3 49.4 %psum.39 = bf16[5,256]{1,0:T(8,128)(2,1)S(1)} all-reduce(bf16[5,256]{1,0:T(8,128)(2,1)} %reduce-scatter.14.cloned.1.call-done), channel_id=1, replica_groups=mesh['seq'=8,'wsh'=4] {'seq'}, use_global_device_ids=true, to_apply=%region_21.23 | all-reduce | flops 1280 | bytes 5120 | tf_op jit(solution)/shard_map/psum | solution.py:177
  756.7 0.6 fusion.63
  757.3 0.9 all-to-all-done.3
  758.3 222.7 %all-reduce.3.cloned.1.call-done = (bf16[256,4608]{1,0:T(8,128)(2,1)}, bf16[256,9216]{1,0:T(8,128)(2,1)}, bf16[256,1024]{1,0:T(8,128)(2,1)}, bf16[256,3072]{1,0:T(8,128)(2,1)}) async-done(((bf16[256,4608]{1,0:T(8,128)(2,1)}, bf16[256,9216]{1,0:T(8,128)(2,1)}, bf16[256,1024]{1,0:T(8,128)(2,1)}, bf16[256,3072]{1,0:T(8,128)(2,1)}), (bf16[256,4608]{1,0:T(8,128)(2,1)}, bf16[256,9216]{1,0:T(8,128)(2,1)}, ...) | async-done | bytes 9175056 | tf_op jit(solution)/shard_map/psum | solution.py:176
  980.9 10.2 convert_multiply_fusion
  991.1 19.2 %mul.433 = f32[2,128,140,128]{3,2,1,0:T(8,128)} reshape(f32[256,17920]{1,0:T(8,128)} %convert_multiply_fusion) | data formatting | bytes 36700160 | tf_op jit(solution)/shard_map/mul | solution.py:180
  1010.3 12.0 %copy.22 = f32[2,140,128,128]{3,2,1,0:T(8,128)S(1)} copy(f32[2,140,128,128]{3,1,2,0:T(8,128)} %bitcast.79) | data formatting | bytes 36700160 | tf_op jit(solution)/shard_map/transpose | solution.py:188
  1022.4 29.2 %fusion.19 = f32[1,280,16,128]{3,2,1,0:T(8,128)S(1)} fusion(f32[2,280,16,128]{3,2,1,0:T(8,128)S(1)} %bitcast.83, f32[280,128,128]{2,1,0:T(8,128)S(1)} %bitcast.76, s32[]{:T(128)S(6)} %select_n.16), kind=kOutput, calls=%fused_computation.39 | convolution fusion | flops 882524160 | bytes 25231364 | tf_op jit(solution)/shard_map/nij,nkj->nik/dot_general | solution.py:195
  1051.6 35.4 %fusion.18 = f32[1,280,16,128]{3,2,1,0:T(8,128)S(1)} fusion(f32[2,280,16,128]{3,2,1,0:T(8,128)S(1)} %bitcast.83, f32[280,128,128]{2,1,0:T(8,128)S(1)} %bitcast.77, s32[]{:T(128)S(6)} %select_n.16), kind=kOutput, calls=%fused_computation.37 | convolution fusion | flops 882524160 | bytes 41287684 | tf_op jit(solution)/shard_map/nji,njk->nik/dot_general | solution.py:196
  1087.0 2.4 pad_maximum_fusion.3
  1089.5 17.0 %fusion.16 = f32[280,128,16]{1,2,0:T(8,128)S(1)} fusion(f32[280,128,128]{2,1,0:T(8,128)S(1)} %bitcast.78, f32[2,280,16,128]{3,2,1,0:T(8,128)} %param.21), kind=kOutput, calls=%fused_computation.34 | convolution fusion | flops 880803840 | bytes 22937600 | tf_op jit(solution)/shard_map/nij,njk->nik/dot_general | solution.py:206
  1106.5 10.2 all-gather.6.cloned.1.call-done
  1116.6 10.6 fusion.54
  1127.3 1.0 copy.31
  1128.2 0.6 copy-done.7
  1128.9 1.0 copy.32
  (105 shorter events, 3.1 us)
Async XLA Ops:
  7.2 8.2 copy-start.23
  7.2 226.6 %all-gather.4.cloned.1.call-start = ((), (), s32[]{:S(2)}) async-start(), calls=%async_computation.9 | async-start | bytes 45875200 | tf_op jit(solution)/shard_map/all_gather | solution.py:82
  7.9 37.7 %copy-start.22 = (bf16[2,256]{1,0:T(2,128)(2,1)S(1)}, bf16[2,256]{1,0:T(2,128)(2,1)}, u32[]{:S(2)}) copy-start(bf16[2,256]{1,0:T(2,128)(2,1)} %param.17) | copy-start | bytes 3076
  7.9 42.9 %copy-start.21 = (bf16[3,256]{1,0:T(4,128)(2,1)S(1)}, bf16[3,256]{1,0:T(4,128)(2,1)}, u32[]{:S(2)}) copy-start(bf16[3,256]{1,0:T(4,128)(2,1)} %param.18) | copy-start | bytes 4612
  7.9 48.2 %copy-start.24 = (s32[8]{0:T(128)S(1)}, s32[8]{0:T(128)}, u32[]{:S(2)}) copy-start(s32[8]{0:T(128)} %param.14) | copy-start | bytes 100
  7.9 33.2 %all-to-all-start = ((bf16[8,64,1024]{2,1,0:T(8,128)(2,1)}), bf16[8,64,1024]{2,1,0:T(8,128)(2,1)S(1)}, u32[]{:S(2)}, u32[]{:S(2)}) async-start(bf16[8,64,1024]{2,1,0:T(8,128)(2,1)} %bitcast), calls=%async_computation | async-start | bytes 2097152 | tf_op jit(solution)/shard_map/all_to_all | solution.py:72
  41.1 29.8 %all-to-all-start.2 = ((bf16[8,64,1024]{2,1,0:T(8,128)(2,1)}), bf16[8,64,1024]{2,1,0:T(8,128)(2,1)}, u32[]{:S(2)}, u32[]{:S(2)}) async-start(bf16[8,64,1024]{2,1,0:T(8,128)(2,1)} %bitcast.10), calls=%async_computation.2 | async-start | bytes 2097152 | tf_op jit(solution)/shard_map/all_to_all | solution.py:75
  45.4 325.4 %reduce-scatter.8.cloned.1.call-start = ((), (), s32[]{:S(2)}) async-start(), calls=%async_computation.11 | async-start | bytes 2621440 | tf_op jit(solution)/shard_map/reduce_scatter | solution.py:159
  74.1 159.7 %copy-start.18 = (bf16[512,1024]{1,0:T(8,128)(2,1)}, bf16[512,1024]{1,0:T(8,128)(2,1)S(1)}, u32[]{:S(2)}) copy-start(bf16[512,1024]{1,0:T(8,128)(2,1)S(1)} %fusion.32) | copy-start | bytes 3145732
  239.3 5.4 copy-start
  239.3 4.2 copy-start.5
  239.8 4.9 collective-permute-start
  247.0 3.3 copy-start.16
  250.3 18.3 %copy-start.10 = (f32[512,1024]{1,0:T(8,128)}, f32[512,1024]{1,0:T(8,128)S(1)}, u32[]{:S(2)}) copy-start(f32[512,1024]{1,0:T(8,128)S(1)} %get-tuple-element.51) | copy-start | bytes 6291460
  286.4 16.0 %copy-start.8 = (bf16[8,64,1024]{2,1,0:T(8,128)(2,1)S(1)}, bf16[8,64,1024]{2,1,0:T(8,128)(2,1)}, u32[]{:S(2)}) copy-start(bf16[8,64,1024]{2,1,0:T(8,128)(2,1)} %broadcast_select_fusion.2) | copy-start | bytes 3145732
  286.4 16.0 %copy-start.11 = (f32[512,1024]{1,0:T(8,128)S(1)}, f32[512,1024]{1,0:T(8,128)}, u32[]{:S(2)}) copy-start(f32[512,1024]{1,0:T(8,128)} %copy-done.10) | copy-start | bytes 6291460
  302.4 2.2 copy-start.17
  303.2 1.5 copy-start.2
  307.3 93.6 %reduce-scatter.6.cloned.1.call-start = ((), (), s32[]{:S(2)}) async-start(), calls=%async_computation.10 | async-start | bytes 7864320 | tf_op jit(solution)/shard_map/reduce_scatter | solution.py:156
  307.3 3.7 copy-start.1
  307.4 12.3 %slice-start = ((s8[6291456]{0:T(1024)(128)(4,1)}), s8[4194304]{0:T(1024)(128)(4,1)S(1)}, s32[]{:S(2)}) async-start(s8[6291456]{0:T(1024)(128)(4,1)} %bitcast.80), calls=%async_computation.17 | async-start | bytes 8388608
  311.0 8.6 slice-start.1
  313.4 9.4 copy-start.13
  313.5 5.8 collective-permute-start.1
  322.2 1.0 copy-start.14
  322.2 2.0 copy-start.19
  322.8 1.0 copy-start.15
  329.9 1.2 copy-start.9
  329.9 151.9 %reduce-scatter.12.cloned.1.call-start = ((), (), s32[]{:S(2)}) async-start(), calls=%async_computation.13 | async-start | bytes 11796480 | tf_op jit(solution)/shard_map/reduce_scatter | solution.py:165
  341.0 1.6 copy-start.12
  341.0 281.2 %reduce-scatter.10.cloned.1.call-start = ((), (), s32[]{:S(2)}) async-start(), calls=%async_computation.12 | async-start | bytes 23592960 | tf_op jit(solution)/shard_map/reduce_scatter | solution.py:162
  360.4 346.9 %reduce-scatter.14.cloned.1.call-start = ((), (), s32[]{:S(2)}) async-start(), calls=%async_computation.14 | async-start | bytes 20480 | tf_op jit(solution)/shard_map/reduce_scatter | solution.py:168
  370.7 610.2 %all-reduce.3.cloned.1.call-start = ((), (), s32[]{:S(2)}) async-start(), calls=%async_computation.16 | async-start | bytes 18350080 | tf_op jit(solution)/shard_map/psum | solution.py:176
  622.2 494.4 %all-gather.6.cloned.1.call-start = ((), (), s32[]{:S(2)}) async-start(), calls=%async_computation.15 | async-start | bytes 10321920 | tf_op jit(solution)/shard_map/all_gather | solution.py:203
  636.0 3.0 copy-start.3
  642.2 1.9 copy-start.4
  645.4 111.4 %copy-start.20 = (f32[5,256]{1,0:T(8,128)S(1)}, f32[5,256]{1,0:T(8,128)}, u32[]{:S(2)}) copy-start(f32[5,256]{1,0:T(8,128)} %param.19) | copy-start | bytes 15364
  703.6 54.7 %all-to-all-start.3 = ((bf16[8,64,1024]{2,1,0:T(8,128)(2,1)}), bf16[8,64,1024]{2,1,0:T(8,128)(2,1)S(1)}, u32[]{:S(2)}, u32[]{:S(2)}) async-start(bf16[8,64,1024]{2,1,0:T(8,128)(2,1)} %get-tuple-element.48), calls=%async_computation.3 | async-start | bytes 2097152 | tf_op jit(solution)/shard_map/all_to_all | solution.py:153
  758.3 222.7 %copy-start.6 = (bf16[8,64,1024]{2,1,0:T(8,128)(2,1)}, bf16[8,64,1024]{2,1,0:T(8,128)(2,1)S(1)}, u32[]{:S(2)}) copy-start(bf16[8,64,1024]{2,1,0:T(8,128)(2,1)S(1)} %all-to-all-done.3) | copy-start | bytes 3145732
  991.1 31.2 %slice-start.2 = ((s8[4587520]{0:T(1024)(128)(4,1)}), s8[393216]{0:T(1024)(128)(4,1)S(1)}, s32[]{:S(2)}) async-start(s8[4587520]{0:T(1024)(128)(4,1)} %bitcast.82), calls=%async_computation.19 | async-start | bytes 786432
  1010.3 12.0 %slice-start.3 = ((s8[4587520]{0:T(1024)(128)(4,1)}), s8[4194304]{0:T(1024)(128)(4,1)S(1)}, s32[]{:S(2)}) async-start(s8[4587520]{0:T(1024)(128)(4,1)} %bitcast.82), calls=%async_computation.20 | async-start | bytes 8388608
  1127.3 1.6 copy-start.7
Sparse Core Ops, SparseCore 0:
  9.6 224.1 all-gather.3
  307.4 31.9 reduce-scatter.7
  342.0 58.8 reduce-scatter.5
  403.9 77.9 reduce-scatter.11
  484.3 137.8 reduce-scatter.9
  625.0 19.4 reduce-scatter.13
  649.1 331.8 all-reduce.2
  983.0 133.6 all-gather.5
where the time goes:
time: 1140 us
  waiting for transfers between devices  689 us (60%)
  matrix products  212 us (19%)
  blocking collectives  118 us (10%)
  local copies, waits for them, and re-layouts  51.4 us (5%)
  other arithmetic  30.2 us (3%)
  starting transfers between devices  20.7 us (2%)
  between operations  14.9 us (1%)
    psum x1, waiting for transfers between devices, shards(): lax.psum(summed[3].astype(jnp.bfloat16), 'seq').astype(jnp.float32)  223 us
    all_gather x1, waiting for transfers between devices, shards(): lax.all_gather(weights, 'wsh', axis=0, tiled=True)  160 us
    reduce_scatter x1, waiting for transfers between devices, shards(): lax.psum_scatter(g_gu.astype(jnp.bfloat16), 'wsh', scatter_dimension=0, t...  140 us
    reduce_scatter x1, waiting for transfers between devices, shards(): lax.psum_scatter(g_down.astype(jnp.bfloat16), 'wsh', scatter_dimension=0,...  81 us
    all_to_all x1, blocking collectives, shards(): lax.all_to_all(leaving[0], 'seq', split_axis=0, concat_axis=0, tiled=True)  58.2 us
    psum x1, blocking collectives, shards(): lax.psum(summed[4].astype(jnp.bfloat16), 'seq').astype(jnp.float32)  49.4 us
    dot_general x4, matrix products, contract_cols(): lax.dot_general(left, right, (((1,), (1,)), ((), ())), preferred_element_...  39.1 us
    dot_general x4, matrix products, contract_rows(): lax.dot_general(left, right, (((0,), (0,)), ((), ())), preferred_element_...  36 us
  transfers between devices with their start and end apart: 13, of which 10 were waited for; matrix products, arithmetic and copies ran while one was open for 18% of the time, Pallas kernels for 0%

commit v1 on v0

--- a/solution.py
+++ b/solution.py
@@ -12,6 +12,19 @@
 LEARN = 0.03
 LEARN_VEC = 0.05
 HIGH = lax.Precision.HIGHEST
+
+
+def ring_gather(array, axis, dim):
+    ways = lax.axis_size(axis)
+    up = [(d, (d + 1) % ways) for d in range(ways)]
+    down = [(d, (d - 1) % ways) for d in range(ways)]
+    earlier, later = ([array], [array])
+    for _ in range(ways // 2):
+        earlier.append(lax.ppermute(earlier[-1], axis, up))
+    for _ in range((ways - 1) // 2):
+        later.append(lax.ppermute(later[-1], axis, down))
+    line = jnp.concatenate([*earlier[::-1], *later[1:]], axis=dim)
+    return jnp.roll(line, (lax.axis_index(axis) - ways // 2) * array.shape[dim], axis=dim)
 
 
 def passed_along(block, axis, distance):
@@ -79,7 +92,7 @@
     x_bf = jnp.take(arrived[0], deal_order, axis=0).reshape(rows, D)
     dy_bf = jnp.take(arrived[1], deal_order, axis=0).reshape(rows, D)
     full_w, gains_bf, kernel_bf = (
-        lax.all_gather(weights, "wsh", axis=0, tiled=True),
+        ring_gather(weights, "wsh", 0),
         lax.all_gather(norm_gains, "wsh", axis=1, tiled=True),
         lax.all_gather(conv_kernel, "wsh", axis=1, tiled=True),
     )

time: 1140 us -> 1290 us (1.13)
  blocking collectives: 118 us -> 276 us
  waiting for transfers between devices: 689 us -> 619 us
  local copies, waits for them, and re-layouts: 51.4 us -> 113 us
    all_gather x1 -> x0, waiting for transfers between devices: 160 us -> none  [shards(): lax.all_gather(weights, 'wsh', axis=0, tiled=True)]
    all_gather x1, blocking collectives: 5.21 us -> 162 us  [shards(): lax.all_gather(norm_gains, 'wsh', axis=1, tiled=True)]
    ppermute x0 -> x3, waiting for transfers between devices: none -> 102 us  [the longest x2 102 us: ring_gather(): earlier.append(lax.ppermute(earlier[-1], axis, up))]
    unnamed x60 -> x75, local copies, waits for them, and re-layouts: 8.24 us -> 63.1 us
    all_to_all x1, waiting for transfers between devices: 13.6 us -> 0.01 us  [shards(): lax.all_to_all(out_grad.reshape(n_seq, unit, D), 'seq', split_axis=0, con...]
  transfers between devices with their start and end apart: 13 -> 15, of which waited for: 10 -> 10; matrix products, arithmetic and copies ran while one was open for 18% -> 18% of each run, Pallas kernels for 0% -> 0%
where the time goes in v1:
time: 1290 us
  waiting for transfers between devices  619 us (48%)
  blocking collectives  276 us (21%)
  matrix products  211 us (16%)
  local copies, waits for them, and re-layouts  113 us (9%)
  other arithmetic  28.1 us (2%)
  starting transfers between devices  22.6 us (2%)
  between operations  15.1 us (1%)
    psum x1, waiting for transfers between devices, shards(): lax.psum(summed[3].astype(jnp.bfloat16), 'seq').astype(jnp.float32)  223 us
    all_gather x1, blocking collectives, shards(): lax.all_gather(norm_gains, 'wsh', axis=1, tiled=True)  162 us
    reduce_scatter x1, waiting for transfers between devices, shards(): lax.psum_scatter(g_gu.astype(jnp.bfloat16), 'wsh', scatter_dimension=0, t...  140 us
    ppermute x2, waiting for transfers between devices, ring_gather(): earlier.append(lax.ppermute(earlier[-1], axis, up))  102 us
    reduce_scatter x1, waiting for transfers between devices, shards(): lax.psum_scatter(g_down.astype(jnp.bfloat16), 'wsh', scatter_dimension=0,...  81.1 us
    unnamed x75, local copies, waits for them, and re-layouts  63.1 us
    all_to_all x1, blocking collectives, shards(): lax.all_to_all(leaving[0], 'seq', split_axis=0, concat_axis=0, tiled=True)  58.3 us
    psum x1, blocking collectives, shards(): lax.psum(summed[4].astype(jnp.bfloat16), 'seq').astype(jnp.float32)  49.4 us
  transfers between devices with their start and end apart: 15, of which 10 were waited for; matrix products, arithmetic and copies ran while one was open for 18% of the time, Pallas kernels for 0%

profile of v1, /device:TPU:0, one launch (start us, length us, event | category | flops | bytes accessed | tf_op | source)
XLA Modules:
  0.0 1285.1 jit_solution(11995519392868290568)
XLA Ops:
  7.7 101.8 %collective-permute-done = bf16[256,17920]{1,0:T(8,128)(2,1)} collective-permute-done((bf16[256,17920]{1,0:T(8,128)(2,1)}, bf16[256,17920]{1,0:T(8,128)(2,1)}, u32[]{:S(2)}, u32[]{:S(2)}) %collective-permute-start) | collective-permute-done | bytes 9175072 | tf_op jit(solution)/shard_map/ppermute | solution.py:23
  109.6 6.6 all-to-all-start
  116.2 1.5 collective-permute-start.2
  117.6 0.8 reduce-window_clone.1
  119.1 24.3 %all-to-all-done = bf16[8,64,1024]{2,1,0:T(8,128)(2,1)S(1)} async-done(((bf16[8,64,1024]{2,1,0:T(8,128)(2,1)}), bf16[8,64,1024]{2,1,0:T(8,128)(2,1)S(1)}, u32[]{:S(2)}, u32[]{:S(2)}) %all-to-all-start) | async-done | bytes 1048608 | tf_op jit(solution)/shard_map/all_to_all | solution.py:85
  143.4 4.2 all-to-all-start.2
  147.8 162.4 %all_gather.9 = bf16[2,1024]{1,0:T(2,128)(2,1)S(1)} all-gather(bf16[2,256]{1,0:T(2,128)(2,1)S(1)} %copy-done.26), channel_id=1, replica_groups=mesh['seq'=8,'wsh'=4] {'wsh'}, dimensions={1}, use_global_device_ids=true | all-gather | bytes 5120 | tf_op jit(solution)/shard_map/all_gather | solution.py:96
  310.2 5.8 all_gather.10
  317.2 1.8 gather_fusion.2
  319.4 8.1 constant_dynamic-update-slice_fusion.7
  327.6 7.8 constant_dynamic-update-slice_fusion.6
  335.3 7.8 constant_dynamic-update-slice_fusion.5
  343.1 7.7 constant_dynamic-update-slice_fusion.4
  350.8 7.6 constant_dynamic-update-slice_fusion.3
  358.5 7.8 constant_dynamic-update-slice_fusion.2
  366.2 7.7 constant_dynamic-update-slice_fusion.1
  374.0 7.7 constant_dynamic-update-slice_fusion
  381.7 5.5 fusion.14
  387.7 4.0 collective-permute-start.3
  391.9 0.7 collective-permute-done.3
  392.7 2.3 multiply_convert_fusion.7
  395.0 3.3 multiply_reduce_fusion.3
  398.4 18.3 %fusion.4 = f32[512,9216]{1,0:T(8,128)} fusion(bf16[2048,17920]{1,0:T(8,128)(2,1)} %constant_dynamic-update-slice_fusion, s32[]{:T(128)S(6)} %select_n.29, s32[]{:T(128)S(6)} %add.141, f32[512,1024]{1,0:T(8,128)S(1)} %get-tuple-element.51, f32[1024]{0:T(1024)S(1)} %bitcast.101, f32[512]{0:T(512)S(1)} %add_rsqrt_fusion.1), kind=kOutput, calls=%fused_computation.10 | convolution fusion | flops 9665249280 | bytes 39852040 | tf_op jit(solution)/shard_map/dot_general | solution.py:123
  416.6 16.8 %multiply_convert_fusion.1 = (bf16[512,4608]{1,0:T(8,128)(2,1)}, bf16[512,4608]{1,0:T(8,128)(2,1)}, bf16[512,4608]{1,0:T(8,128)(2,1)}) fusion(f32[512,9216]{1,0:T(8,128)} %fusion.4, bf16[512,1024]{1,0:T(8,128)(2,1)S(1)} %bitcast.86, bf16[2048,17920]{1,0:T(8,128)(2,1)} %constant_dynamic-update-slice_fusion, s32[]{:T(128)S(6)} %select_n.29, s32[]{:T(128)S(6)} %add.142), kind=kOutput, calls=%fused_computation.15 | convolution fusion | flops 4869586944 | bytes 43515912 | tf_op jit(solution)/shard_map/dot_general | solution.py:131
  433.4 15.9 %multiply_reduce_fusion.1 = (bf16[1024]{0:T(1024)(128)(2,1)S(1)}, f32[512]{0:T(512)S(1)}, f32[512,1024]{1,0:T(8,128)S(1)}) fusion(f32[512,1024]{1,0:T(8,128)} %copy-done.10, f32[512]{0:T(512)S(1)} %add_rsqrt_fusion.1, f32[1024]{0:T(1024)S(1)} %bitcast.102, bf16[2048,17920]{1,0:T(8,128)(2,1)} %constant_dynamic-update-slice_fusion, s32[]{:T(128)S(6)} %select_n.29, ...), kind=kOutput, calls=%fused_computation.75 | convolution fusion | flops 9685694464 | bytes 32516104 | tf_op jit(solution)/shard_map/dot_general | solution.py:63
  449.4 0.7 subtract_add_fusion
  450.1 1.3 copy-done.3
  451.4 2.6 convolution_convert_fusion.3
  454.1 4.9 multiply_convert_fusion.4
  459.1 1.6 collective-permute-start.4
  460.6 4.5 collective-permute-done.4
  465.5 2.6 fusion.26
  470.1 5.8 convolution_convert_fusion.2
  475.9 1.1 copy-done.9
  477.1 9.8 convolution_convert_fusion.1
  487.0 1.5 copy-done.12
  488.5 17.3 %convolution_convert_fusion = bf16[1024,9216]{1,0:T(8,128)(2,1)} fusion(bf16[512,4608]{1,0:T(8,128)(2,1)} %get-tuple-element.32, bf16[512,4608]{1,0:T(8,128)(2,1)} %get-tuple-element.31, f32[512,1024]{1,0:T(8,128)S(1)} %copy-done.12, f32[1024]{0:T(1024)S(1)} %bitcast.104, f32[512]{0:T(512)S(1)} %add_rsqrt_fusion.1), kind=kOutput, calls=%fused_computation.7 | convolution fusion | flops 9693560832 | bytes 30414848 | tf_op jit(solution)/shard_map/dot_general | solution.py:57
  506.5 8.8 fusion.41
  516.1 32.7 %reduce-scatter.6.cloned.1.call-done = bf16[256,3072]{1,0:T(8,128)(2,1)} async-done(((bf16[1024,3072]{1,0:T(8,128)(2,1)}), bf16[256,3072]{1,0:T(8,128)(2,1)}) %reduce-scatter.6.cloned.1.call-update) | async-done | bytes 1572880 | tf_op jit(solution)/shard_map/reduce_scatter | solution.py:169
  548.8 81.1 %reduce-scatter.12.cloned.1.call-done = bf16[256,4608]{1,0:T(8,128)(2,1)} async-done(((bf16[1024,4608]{1,0:T(8,128)(2,1)}), bf16[256,4608]{1,0:T(8,128)(2,1)}) %reduce-scatter.12.cloned.1.call-update) | async-done | bytes 2359312 | tf_op jit(solution)/shard_map/reduce_scatter | solution.py:178
  630.0 140.3 %reduce-scatter.10.cloned.1.call-done = bf16[256,9216]{1,0:T(8,128)(2,1)} async-done(((bf16[1024,9216]{1,0:T(8,128)(2,1)}), bf16[256,9216]{1,0:T(8,128)(2,1)}) %reduce-scatter.10.cloned.1.call-update) | async-done | bytes 4718608 | tf_op jit(solution)/shard_map/reduce_scatter | solution.py:175
  770.4 2.8 slice.226
  773.2 1.0 sort.17
  774.2 9.9 add_convert_fusion
  784.0 3.0 gather_fusion.1
  787.0 3.3 fusion.37
  790.3 1.9 gather_fusion.3
  792.2 1.2 broadcast_select_fusion
  793.5 58.3 %all_to_all.20 = bf16[8,64,1024]{2,1,0:T(8,128)(2,1)S(1)} all-to-all(bf16[8,64,1024]{2,1,0:T(8,128)(2,1)S(1)} %get-tuple-element.49), channel_id=1, replica_groups=mesh['seq'=8,'wsh'=4] {'seq'}, dimensions={0} | all-to-all | bytes 2097152 | tf_op jit(solution)/shard_map/all_to_all | solution.py:165
  851.7 3.7 all-to-all-start.3
  855.5 49.4 %psum.39 = bf16[5,256]{1,0:T(8,128)(2,1)S(1)} all-reduce(bf16[5,256]{1,0:T(8,128)(2,1)} %reduce-scatter.14.cloned.1.call-done), channel_id=1, replica_groups=mesh['seq'=8,'wsh'=4] {'seq'}, use_global_device_ids=true, to_apply=%region_21.23 | all-reduce | flops 1280 | bytes 5120 | tf_op jit(solution)/shard_map/psum | solution.py:190
  905.5 0.9 all-to-all-done.3
  906.4 222.6 %all-reduce.3.cloned.1.call-done = (bf16[256,4608]{1,0:T(8,128)(2,1)}, bf16[256,9216]{1,0:T(8,128)(2,1)}, bf16[256,1024]{1,0:T(8,128)(2,1)}, bf16[256,3072]{1,0:T(8,128)(2,1)}) async-done(((bf16[256,4608]{1,0:T(8,128)(2,1)}, bf16[256,9216]{1,0:T(8,128)(2,1)}, bf16[256,1024]{1,0:T(8,128)(2,1)}, bf16[256,3072]{1,0:T(8,128)(2,1)}), (bf16[256,4608]{1,0:T(8,128)(2,1)}, bf16[256,9216]{1,0:T(8,128)(2,1)}, ...) | async-done | bytes 9175056 | tf_op jit(solution)/shard_map/psum | solution.py:189
  1129.0 10.2 convert_multiply_fusion
  1139.2 19.2 %mul.437 = f32[2,128,140,128]{3,2,1,0:T(8,128)} reshape(f32[256,17920]{1,0:T(8,128)} %convert_multiply_fusion) | data formatting | bytes 36700160 | tf_op jit(solution)/shard_map/mul | solution.py:193
  1158.3 12.0 copy.22
  1170.4 29.5 %fusion.19 = f32[1,280,16,128]{3,2,1,0:T(8,128)S(1)} fusion(f32[2,280,16,128]{3,2,1,0:T(8,128)S(1)} %bitcast.83, f32[280,128,128]{2,1,0:T(8,128)S(1)} %bitcast.76, s32[]{:T(128)S(6)} %select_n.31), kind=kOutput, calls=%fused_computation.39 | convolution fusion | flops 882524160 | bytes 25231364 | tf_op jit(solution)/shard_map/nij,nkj->nik/dot_general | solution.py:208
  1199.9 35.2 %fusion.18 = f32[1,280,16,128]{3,2,1,0:T(8,128)S(1)} fusion(f32[2,280,16,128]{3,2,1,0:T(8,128)S(1)} %bitcast.83, f32[280,128,128]{2,1,0:T(8,128)S(1)} %bitcast.77, s32[]{:T(128)S(6)} %select_n.31), kind=kOutput, calls=%fused_computation.37 | convolution fusion | flops 882524160 | bytes 41287684 | tf_op jit(solution)/shard_map/nji,njk->nik/dot_general | solution.py:209
  1235.1 2.4 pad_maximum_fusion.3
  1237.5 17.0 %fusion.16 = f32[280,128,16]{1,2,0:T(8,128)S(1)} fusion(f32[280,128,128]{2,1,0:T(8,128)S(1)} %bitcast.78, f32[2,280,16,128]{3,2,1,0:T(8,128)} %param.21), kind=kOutput, calls=%fused_computation.34 | convolution fusion | flops 880803840 | bytes 22937600 | tf_op jit(solution)/shard_map/nij,njk->nik/dot_general | solution.py:219
  1254.5 10.2 all-gather.3.cloned.1.call-done
  1264.7 10.6 fusion.52
  1275.3 1.0 copy.38
  1276.9 1.0 copy.39
  (123 shorter events, 8.8 us)
Async XLA Ops:
  7.2 140.6 %copy-start.26 = (bf16[2,256]{1,0:T(2,128)(2,1)S(1)}, bf16[2,256]{1,0:T(2,128)(2,1)}, u32[]{:S(2)}) copy-start(bf16[2,256]{1,0:T(2,128)(2,1)} %param.17) | copy-start | bytes 3076
  7.2 303.1 %copy-start.25 = (bf16[3,256]{1,0:T(4,128)(2,1)S(1)}, bf16[3,256]{1,0:T(4,128)(2,1)}, u32[]{:S(2)}) copy-start(bf16[3,256]{1,0:T(4,128)(2,1)} %param.18) | copy-start | bytes 4612
  7.2 308.8 %copy-start.27 = (s32[8]{0:T(128)S(1)}, s32[8]{0:T(128)}, u32[]{:S(2)}) copy-start(s32[8]{0:T(128)} %param.14) | copy-start | bytes 100
  7.2 102.4 %collective-permute-start = (bf16[256,17920]{1,0:T(8,128)(2,1)}, bf16[256,17920]{1,0:T(8,128)(2,1)}, u32[]{:S(2)}, u32[]{:S(2)}) collective-permute-start(bf16[256,17920]{1,0:T(8,128)(2,1)} %param.16), channel_id=1, source_target_pairs={{0,1},{1,2},{2,3},{3,0},{4,5},{5,6},{6,7},{7,4},{8,9},{9,10},{10,1... | collective-permute-start | bytes 27525128 | tf_op jit(solution)/shard_map/ppermute | solution.py:23
  109.6 209.9 %collective-permute-start.1 = (bf16[256,17920]{1,0:T(8,128)(2,1)}, bf16[256,17920]{1,0:T(8,128)(2,1)}, u32[]{:S(2)}, u32[]{:S(2)}) collective-permute-start(bf16[256,17920]{1,0:T(8,128)(2,1)} %collective-permute-done), channel_id=1, source_target_pairs={{0,1},{1,2},{2,3},{3,0},{4,5},{5,6},{6,7},{7,4},{8,9},{9,10},{10,1... | collective-permute-start | bytes 27525128 | tf_op jit(solution)/shard_map/ppermute | solution.py:23
  109.6 33.8 %all-to-all-start = ((bf16[8,64,1024]{2,1,0:T(8,128)(2,1)}), bf16[8,64,1024]{2,1,0:T(8,128)(2,1)S(1)}, u32[]{:S(2)}, u32[]{:S(2)}) async-start(bf16[8,64,1024]{2,1,0:T(8,128)(2,1)} %bitcast.90), calls=%async_computation | async-start | bytes 2097152 | tf_op jit(solution)/shard_map/all_to_all | solution.py:85
  116.2 227.0 %collective-permute-start.2 = (bf16[256,17920]{1,0:T(8,128)(2,1)}, bf16[256,17920]{1,0:T(8,128)(2,1)}, u32[]{:S(2)}, u32[]{:S(2)}) collective-permute-start(bf16[256,17920]{1,0:T(8,128)(2,1)} %param.16), channel_id=1, source_target_pairs={{0,3},{1,0},{2,1},{3,2},{4,7},{5,4},{6,5},{7,6},{8,11},{9,8},{10,9... | collective-permute-start | bytes 27525128 | tf_op jit(solution)/shard_map/ppermute | solution.py:25
  143.4 173.9 %all-to-all-start.2 = ((bf16[8,64,1024]{2,1,0:T(8,128)(2,1)}), bf16[8,64,1024]{2,1,0:T(8,128)(2,1)}, u32[]{:S(2)}, u32[]{:S(2)}) async-start(bf16[8,64,1024]{2,1,0:T(8,128)(2,1)} %bitcast.91), calls=%async_computation.2 | async-start | bytes 2097152 | tf_op jit(solution)/shard_map/all_to_all | solution.py:88
  147.6 368.5 %reduce-scatter.8.cloned.1.call-start = ((), (), s32[]{:S(2)}) async-start(), calls=%async_computation.10 | async-start | bytes 2621440 | tf_op jit(solution)/shard_map/reduce_scatter | solution.py:172
  316.0 3.0 copy-start.20
  317.2 10.3 copy-start.22
  319.4 62.3 %copy-start.18 = (bf16[512,1024]{1,0:T(8,128)(2,1)}, bf16[512,1024]{1,0:T(8,128)(2,1)S(1)}, u32[]{:S(2)}) copy-start(bf16[512,1024]{1,0:T(8,128)(2,1)S(1)} %fusion.32) | copy-start | bytes 3145732
  387.2 5.4 copy-start
  387.7 7.3 copy-start.1
  387.7 4.9 collective-permute-start.3
  391.9 57.4 %copy-start.8 = (bf16[8,64,1024]{2,1,0:T(8,128)(2,1)}, bf16[8,64,1024]{2,1,0:T(8,128)(2,1)S(1)}, u32[]{:S(2)}) copy-start(bf16[8,64,1024]{2,1,0:T(8,128)(2,1)S(1)} %broadcast_select_fusion.2) | copy-start | bytes 3145732
  395.0 3.3 copy-start.16
  398.3 18.3 %copy-start.10 = (f32[512,1024]{1,0:T(8,128)}, f32[512,1024]{1,0:T(8,128)S(1)}, u32[]{:S(2)}) copy-start(f32[512,1024]{1,0:T(8,128)S(1)} %get-tuple-element.51) | copy-start | bytes 6291460
  433.4 15.9 %copy-start.11 = (f32[512,1024]{1,0:T(8,128)S(1)}, f32[512,1024]{1,0:T(8,128)}, u32[]{:S(2)}) copy-start(f32[512,1024]{1,0:T(8,128)} %copy-done.10) | copy-start | bytes 6291460
  449.4 2.0 copy-start.17
  450.1 1.3 copy-start.3
  451.4 14.1 %slice-start = ((s8[6291456]{0:T(1024)(128)(4,1)}), s8[2097152]{0:T(1024)(128)(4,1)S(1)}, s32[]{:S(2)}) async-start(s8[6291456]{0:T(1024)(128)(4,1)} %bitcast.80), calls=%async_computation.16 | async-start | bytes 4194304
  454.0 94.8 %reduce-scatter.6.cloned.1.call-start = ((), (), s32[]{:S(2)}) async-start(), calls=%async_computation.9 | async-start | bytes 7864320 | tf_op jit(solution)/shard_map/reduce_scatter | solution.py:169
  454.1 11.4 slice-start.1
  459.0 9.6 copy-start.13
  459.0 6.5 copy-start.2
  459.1 6.1 collective-permute-start.4
  468.1 1.0 copy-start.14
  468.1 2.0 copy-start.19
  468.6 1.0 copy-start.15
  475.9 1.2 copy-start.9
  475.9 154.1 %reduce-scatter.12.cloned.1.call-start = ((), (), s32[]{:S(2)}) async-start(), calls=%async_computation.12 | async-start | bytes 11796480 | tf_op jit(solution)/shard_map/reduce_scatter | solution.py:178
  486.9 1.6 copy-start.12
  486.9 283.3 %reduce-scatter.10.cloned.1.call-start = ((), (), s32[]{:S(2)}) async-start(), calls=%async_computation.11 | async-start | bytes 23592960 | tf_op jit(solution)/shard_map/reduce_scatter | solution.py:175
  505.8 0.7 copy-start.21
  505.9 0.7 copy-start.23
  505.9 349.6 %reduce-scatter.14.cloned.1.call-start = ((), (), s32[]{:S(2)}) async-start(), calls=%async_computation.13 | async-start | bytes 20480 | tf_op jit(solution)/shard_map/reduce_scatter | solution.py:181
  516.0 612.9 %all-reduce.3.cloned.1.call-start = ((), (), s32[]{:S(2)}) async-start(), calls=%async_computation.15 | async-start | bytes 18350080 | tf_op jit(solution)/shard_map/psum | solution.py:189
  770.3 2.9 copy-start.28
  770.3 494.4 %all-gather.3.cloned.1.call-start = ((), (), s32[]{:S(2)}) async-start(), calls=%async_computation.14 | async-start | bytes 10321920 | tf_op jit(solution)/shard_map/all_gather | solution.py:216
  784.0 3.0 copy-start.4
  790.3 1.9 copy-start.5
  793.4 111.4 %copy-start.24 = (f32[5,256]{1,0:T(8,128)S(1)}, f32[5,256]{1,0:T(8,128)}, u32[]{:S(2)}) copy-start(f32[5,256]{1,0:T(8,128)} %param.19) | copy-start | bytes 15364
  851.7 54.6 %all-to-all-start.3 = ((bf16[8,64,1024]{2,1,0:T(8,128)(2,1)}), bf16[8,64,1024]{2,1,0:T(8,128)(2,1)S(1)}, u32[]{:S(2)}, u32[]{:S(2)}) async-start(bf16[8,64,1024]{2,1,0:T(8,128)(2,1)} %get-tuple-element.48), calls=%async_computation.3 | async-start | bytes 2097152 | tf_op jit(solution)/shard_map/all_to_all | solution.py:166
  906.4 222.6 %copy-start.6 = (bf16[8,64,1024]{2,1,0:T(8,128)(2,1)}, bf16[8,64,1024]{2,1,0:T(8,128)(2,1)S(1)}, u32[]{:S(2)}) copy-start(bf16[8,64,1024]{2,1,0:T(8,128)(2,1)S(1)} %all-to-all-done.3) | copy-start | bytes 3145732
  1139.2 31.2 %slice-start.2 = ((s8[4587520]{0:T(1024)(128)(4,1)}), s8[393216]{0:T(1024)(128)(4,1)S(1)}, s32[]{:S(2)}) async-start(s8[4587520]{0:T(1024)(128)(4,1)} %bitcast.82), calls=%async_computation.18 | async-start | bytes 786432
  1158.3 12.0 slice-start.3
  1275.3 1.6 copy-start.7
Sparse Core Ops, SparseCore 0:
  454.2 33.2 reduce-scatter.7
  489.9 58.8 reduce-scatter.5
  552.0 77.9 reduce-scatter.11
  632.4 137.8 reduce-scatter.9
  773.1 19.5 reduce-scatter.13
  797.0 331.8 all-reduce.2
  1131.0 133.6 all-gather.2
